TPU v7x, 16 devices: a whole 2x2x2 slice. The times are simulated.
16 devices in a mesh: z: 2 (over z), y: 2 (over y), xc: 4 (over x, core).
Axes of the slice: x: 2, y: 2, z: 2, core: 2. Of those that a mesh axis runs over, the one named last changes fastest.
Arguments:
- tokens_x: bfloat16 [131072, 768], P(('z', 'y', 'xc'))
- grad_y: bfloat16 [131072, 768], P(('z', 'y', 'xc'))
- w_one: bfloat16 [768, 3072], replicated
- w_two: bfloat16 [3072, 768], replicated
- w_three: bfloat16 [768, 3072], replicated
- w_four: bfloat16 [3072, 768], replicated
Outputs:
- output 1: float32 [768, 3072], replicated
- output 2: float32 [3072, 768], replicated
- output 3: float32 [768, 3072], replicated
- output 4: float32 [3072, 768], replicated
All inputs are finite; a program needn't handle non-finite values.
Results may differ from a plain program's by a relative error of at most 0.00304.
Values are sent between devices in bfloat16 or wider.
A program may use at most 1 GiB of HBM per device.

v0:
```python
import math
import jax
import jax.numpy as jnp
from jax import lax
from jax.sharding import PartitionSpec as P

GELU_SCALE = math.sqrt(2.0 / math.pi)
GELU_CUBIC = 0.044715


def gelu_value(pre_act):
    return 0.5 * pre_act * (1.0 + jnp.tanh(GELU_SCALE * (pre_act + GELU_CUBIC * pre_act * pre_act * pre_act)))


def gelu_grad(pre_act):
    tanh_val = jnp.tanh(GELU_SCALE * (pre_act + GELU_CUBIC * pre_act * pre_act * pre_act))
    return 0.5 * (1.0 + tanh_val) + 0.5 * pre_act * (1.0 - tanh_val * tanh_val) * GELU_SCALE * (1.0 + 3.0 * GELU_CUBIC * pre_act * pre_act)


def solution(mesh):
    n_dev = math.prod(mesh.shape.values())
    batch_spec = P(("z", "y", "xc"), None)
    whole_spec = P(None, None)

    def reduce_grad(local_grad):
        reduced = lax.psum_scatter(local_grad, "xc", scatter_dimension=0, tiled=True)
        reduced = lax.psum_scatter(reduced, "y", scatter_dimension=0, tiled=True)
        reduced = lax.psum(reduced, "z")
        reduced = lax.all_gather(reduced, "y", axis=0, tiled=True)
        reduced = lax.all_gather(reduced, "xc", axis=0, tiled=True)
        return reduced / n_dev

    def device_step(x_loc, g_loc, w_one, w_two, w_three, w_four):
        a_one = jnp.dot(x_loc, w_one, preferred_element_type=jnp.float32).astype(jnp.bfloat16)
        h_one = gelu_value(a_one.astype(jnp.float32)).astype(jnp.bfloat16)
        h_two = (jnp.dot(h_one, w_two, preferred_element_type=jnp.float32) + x_loc.astype(jnp.float32)).astype(jnp.bfloat16)
        a_three = jnp.dot(h_two, w_three, preferred_element_type=jnp.float32).astype(jnp.bfloat16)
        h_three = gelu_value(a_three.astype(jnp.float32)).astype(jnp.bfloat16)
        grad_w4 = reduce_grad(jnp.einsum("nf,nd->fd", h_three, g_loc, preferred_element_type=jnp.float32))
        d_a3 = (jnp.einsum("nd,fd->nf", g_loc, w_four, preferred_element_type=jnp.float32) * gelu_grad(a_three.astype(jnp.float32))).astype(jnp.bfloat16)
        grad_w3 = reduce_grad(jnp.einsum("nd,nf->df", h_two, d_a3, preferred_element_type=jnp.float32))
        d_h2 = (jnp.einsum("nf,df->nd", d_a3, w_three, preferred_element_type=jnp.float32) + g_loc.astype(jnp.float32)).astype(jnp.bfloat16)
        grad_w2 = reduce_grad(jnp.einsum("nf,nd->fd", h_one, d_h2, preferred_element_type=jnp.float32))
        d_a1 = (jnp.einsum("nd,fd->nf", d_h2, w_two, preferred_element_type=jnp.float32) * gelu_grad(a_one.astype(jnp.float32))).astype(jnp.bfloat16)
        grad_w1 = reduce_grad(jnp.einsum("nd,nf->df", x_loc, d_a1, preferred_element_type=jnp.float32))
        return grad_w1, grad_w2, grad_w3, grad_w4

    return jax.shard_map(
        device_step,
        mesh=mesh,
        in_specs=(batch_spec, batch_spec, whole_spec, whole_spec, whole_spec, whole_spec),
        out_specs=(whole_spec, whole_spec, whole_spec, whole_spec),
        check_vma=False,
    )
```

profile of v0, /device:TPU:0, one launch (start us, length us, event | category | flops | bytes accessed | tf_op | source)
XLA Modules:
  0.0 1434.2 jit_solution(7058295019296024)
XLA Ops:
  7.2 0.0 reduce-scatter.29.cloned.1.call-start
  7.2 47.2 %convolution_convert_fusion.1 = bf16[8192,3072]{1,0:T(8,128)(2,1)} fusion(bf16[8192,768]{1,0:T(8,128)(2,1)} %param.6, bf16[768,3072]{1,0:T(8,128)(2,1)} %param.8), kind=kOutput, calls=%fused_computation.38 | convolution fusion | flops 38679871488 | bytes 67633152 | tf_op jit(solution)/shard_map/dot_general | solution.py:34
  54.4 69.6 %add_convert_fusion.1 = bf16[8192,768]{1,0:T(8,128)(2,1)} fusion(bf16[8192,768]{1,0:T(8,128)(2,1)} %param.6, bf16[3072,768]{1,0:T(8,128)(2,1)S(1)} %copy-done.1, bf16[8192,3072]{1,0:T(8,128)(2,1)} %convolution_convert_fusion.1), kind=kOutput, calls=%fused_computation.40 | convolution fusion | flops 38925238272 | bytes 80216064 | tf_op jit(solution)/shard_map/dot_general | solution.py:36
  124.1 47.5 %convolution_convert_fusion = bf16[8192,3072]{1,0:T(8,128)(2,1)} fusion(bf16[8192,768]{1,0:T(8,128)(2,1)} %add_convert_fusion.1, bf16[768,3072]{1,0:T(8,128)(2,1)} %param.10), kind=kOutput, calls=%fused_computation.37 | convolution fusion | flops 38679871488 | bytes 67633152 | tf_op jit(solution)/shard_map/dot_general | solution.py:37
  171.6 92.7 %fusion.8 = bf16[8192,3072]{1,0:T(8,128)(2,1)} fusion(bf16[8192,3072]{1,0:T(8,128)(2,1)} %convolution_convert_fusion, bf16[8192,768]{1,0:T(8,128)(2,1)} %param.7, bf16[3072,768]{1,0:T(8,128)(2,1)S(1)} %copy-done), kind=kOutput, calls=%fused_computation.22 | convolution fusion | flops 39158022144 | bytes 117964800 | tf_op jit(solution)/shard_map/nd,fd->nf/dot_general | solution.py:40
  264.3 48.3 %fusion.38 = f32[768,3072]{1,0:T(8,128)} fusion(bf16[8192,768]{1,0:T(8,128)(2,1)} %add_convert_fusion.1, bf16[8192,3072]{1,0:T(8,128)(2,1)} %fusion.8), kind=kOutput, calls=%fused_computation.57 | convolution fusion | flops 38654705664 | bytes 72351744
  312.7 0.0 reduce-scatter.29.cloned.1.call-update
  312.7 0.0 reduce-scatter.25.cloned.1.call-start
  312.7 47.5 %add_convert_fusion = bf16[8192,768]{1,0:T(8,128)(2,1)} fusion(bf16[8192,768]{1,0:T(8,128)(2,1)} %param.7, bf16[8192,3072]{1,0:T(8,128)(2,1)} %fusion.8, bf16[768,3072]{1,0:T(8,128)(2,1)} %param.10), kind=kOutput, calls=%fused_computation.39 | convolution fusion | flops 38673580032 | bytes 80216064 | tf_op jit(solution)/shard_map/nf,df->nd/dot_general | solution.py:42
  360.2 94.0 %fusion.15.clone.6 = bf16[8192,3072]{1,0:T(8,128)(2,1)} fusion(bf16[8192,3072]{1,0:T(8,128)(2,1)} %convolution_convert_fusion.1, bf16[8192,768]{1,0:T(8,128)(2,1)} %add_convert_fusion, bf16[3072,768]{1,0:T(8,128)(2,1)} %param.9), kind=kOutput, calls=%fused_computation.29.clone.clone.clone.clone.clone.1 | convolution fusion | flops 39158022144 | bytes 117964800 | tf_op jit(solution)/shard_map/nd,fd->nf/dot_general | solution.py:44
  454.2 48.7 %fusion.25 = f32[768,3072]{0,1:T(8,128)} fusion(bf16[8192,768]{1,0:T(8,128)(2,1)} %param.6, bf16[8192,3072]{1,0:T(8,128)(2,1)} %fusion.15.clone.6), kind=kOutput, calls=%fused_computation.42 | convolution fusion | flops 38654705664 | bytes 72351744 | tf_op jit(solution)/shard_map/nd,nf->df/dot_general | solution.py:45
  502.9 9.6 copy.17
  512.5 0.0 reduce-scatter.21.cloned.1.call-start
  512.5 63.2 %fusion.22 = f32[3072,768]{1,0:T(8,128)} fusion(bf16[8192,768]{1,0:T(8,128)(2,1)} %param.7, bf16[8192,3072]{1,0:T(8,128)(2,1)} %convolution_convert_fusion), kind=kOutput, calls=%fused_computation.36 | convolution fusion | flops 38906363904 | bytes 72351744 | tf_op jit(solution)/shard_map/nf,nd->fd/dot_general | solution.py:39
  575.8 0.0 reduce-scatter.17.cloned.1.call-start
  575.8 63.4 %fusion.35 = f32[3072,768]{1,0:T(8,128)} fusion(bf16[8192,768]{1,0:T(8,128)(2,1)} %add_convert_fusion, bf16[8192,3072]{1,0:T(8,128)(2,1)} %convolution_convert_fusion.1), kind=kOutput, calls=%fused_computation.56 | convolution fusion | flops 38906363904 | bytes 72351744 | tf_op jit(solution)/shard_map/nf,nd->fd/dot_general | solution.py:43
  639.2 0.0 reduce-scatter.17.cloned.1.call-update
  639.3 0.0 reduce-scatter.31.cloned.1.call-start
  639.3 0.0 reduce-scatter.29.cloned.1.call-done
  639.3 0.5 reduce-scatter.31.cloned.1.call-update
  639.9 0.0 reduce-scatter.27.cloned.1.call-start
  639.9 0.0 reduce-scatter.25.cloned.1.call-done
  639.9 0.5 reduce-scatter.27.cloned.1.call-update
  640.4 0.0 reduce-scatter.23.cloned.1.call-start
  640.5 24.8 %reduce-scatter.21.cloned.1.call-done = f32[768,768]{1,0:T(8,128)} async-done(((f32[3072,768]{1,0:T(8,128)}), f32[768,768]{1,0:T(8,128)}) %reduce-scatter.21.cloned.1.call-update) | async-done | bytes 2359312 | tf_op jit(solution)/shard_map/reduce_scatter | solution.py:26
  665.3 0.0 reduce-scatter.23.cloned.1.call-update
  665.3 0.0 reduce-scatter.19.cloned.1.call-start
  665.4 76.3 %reduce-scatter.17.cloned.1.call-done = f32[768,768]{1,0:T(8,128)} async-done(((f32[3072,768]{1,0:T(8,128)}), f32[768,768]{1,0:T(8,128)}) %reduce-scatter.17.cloned.1.call-update) | async-done | bytes 2359312 | tf_op jit(solution)/shard_map/reduce_scatter | solution.py:26
  741.7 0.0 reduce-scatter.19.cloned.1.call-update
  741.7 0.0 all-reduce.3.cloned.1.call-start
  741.8 34.9 %reduce-scatter.31.cloned.1.call-done = f32[96,3072]{1,0:T(8,128)} async-done(((f32[192,3072]{1,0:T(8,128)}), f32[96,3072]{1,0:T(8,128)}) %reduce-scatter.31.cloned.1.call-update) | async-done | bytes 1179664
  776.6 2.9 copy.24
  779.5 32.0 %reduce-scatter.27.cloned.1.call-done = f32[96,3072]{1,0:T(8,128)} async-done(((f32[192,3072]{1,0:T(8,128)}), f32[96,3072]{1,0:T(8,128)}) %reduce-scatter.27.cloned.1.call-update) | async-done | bytes 1179664
  811.6 2.9 copy.20
  814.5 32.2 %reduce-scatter.23.cloned.1.call-done = f32[384,768]{1,0:T(8,128)} async-done(((f32[768,768]{1,0:T(8,128)}), f32[384,768]{1,0:T(8,128)}) %reduce-scatter.23.cloned.1.call-update) | async-done | bytes 1179664 | tf_op jit(solution)/shard_map/reduce_scatter | solution.py:27
  846.6 35.1 %reduce-scatter.19.cloned.1.call-done = f32[384,768]{1,0:T(8,128)} async-done(((f32[768,768]{1,0:T(8,128)}), f32[384,768]{1,0:T(8,128)}) %reduce-scatter.19.cloned.1.call-update) | async-done | bytes 1179664 | tf_op jit(solution)/shard_map/reduce_scatter | solution.py:27
  881.7 0.0 all-reduce.3.cloned.1.call-update
  881.7 0.0 all-gather.9.cloned.1.call-start
  881.8 135.5 %all-reduce.3.cloned.1.call-done = (f32[96,3072]{0,1:T(8,128)}, f32[384,768]{1,0:T(8,128)}, f32[96,3072]{0,1:T(8,128)}, f32[384,768]{1,0:T(8,128)}) async-done(((f32[96,3072]{0,1:T(8,128)}, f32[384,768]{1,0:T(8,128)}, f32[96,3072]{0,1:T(8,128)}, f32[384,768]{1,0:T(8,128)}), (f32[96,3072]{0,1:T(8,128)}, f32[384,768]{1,0:T(8,128)}, f32[96,3072]{0,1:T(8,128)}, ...) | async-done | bytes 4718608 | tf_op jit(solution)/shard_map/psum | solution.py:28
  1017.3 2.9 copy.13
  1020.2 0.0 all-gather.9.cloned.1.call-update
  1020.2 0.0 all-gather.13.cloned.1.call-start
  1020.3 0.7 all-gather.13.cloned.1.call-update
  1020.9 0.0 all-gather.21.cloned.1.call-start
  1021.0 0.5 all-gather.21.cloned.1.call-update
  1021.5 0.0 all-gather.17.cloned.1.call-start
  1021.6 2.9 copy.15
  1024.5 0.0 all-gather.17.cloned.1.call-update
  1024.5 0.0 all-gather.11.cloned.1.call-start
  1024.5 29.9 %all-gather.9.cloned.1.call-done = f32[192,3072]{1,0:T(8,128)} async-done(((f32[96,3072]{1,0:T(8,128)}), f32[192,3072]{1,0:T(8,128)}) %all-gather.9.cloned.1.call-update) | async-done | bytes 2359312 | tf_op jit(solution)/shard_map/all_gather | solution.py:29
  1054.4 0.0 all-gather.15.cloned.1.call-start
  1054.5 35.5 %all-gather.13.cloned.1.call-done = f32[768,768]{1,0:T(8,128)} async-done(((f32[384,768]{1,0:T(8,128)}), f32[768,768]{1,0:T(8,128)}) %all-gather.13.cloned.1.call-update) | async-done | bytes 2359312 | tf_op jit(solution)/shard_map/all_gather | solution.py:29
  1090.0 0.0 all-gather.23.cloned.1.call-start
  1090.1 35.4 %all-gather.21.cloned.1.call-done = f32[768,768]{1,0:T(8,128)} async-done(((f32[384,768]{1,0:T(8,128)}), f32[768,768]{1,0:T(8,128)}) %all-gather.21.cloned.1.call-update) | async-done | bytes 2359312 | tf_op jit(solution)/shard_map/all_gather | solution.py:29
  1125.5 0.0 all-gather.19.cloned.1.call-start
  1125.6 36.1 %all-gather.17.cloned.1.call-done = f32[192,3072]{1,0:T(8,128)} async-done(((f32[96,3072]{1,0:T(8,128)}), f32[192,3072]{1,0:T(8,128)}) %all-gather.17.cloned.1.call-update) | async-done | bytes 2359312 | tf_op jit(solution)/shard_map/all_gather | solution.py:29
  1161.7 64.1 %all-gather.11.cloned.1.call-done = f32[768,3072]{1,0:T(8,128)} async-done(((f32[192,3072]{1,0:T(8,128)}), f32[768,3072]{1,0:T(8,128)}) %all-gather.11.cloned.1.call-update) | async-done | bytes 9437200 | tf_op jit(solution)/shard_map/all_gather | solution.py:30
  1225.8 9.1 broadcast_multiply_fusion.3
  1234.9 55.0 %all-gather.15.cloned.1.call-done = f32[3072,768]{1,0:T(8,128)} async-done(((f32[768,768]{1,0:T(8,128)}), f32[3072,768]{1,0:T(8,128)}) %all-gather.15.cloned.1.call-update) | async-done | bytes 9437200 | tf_op jit(solution)/shard_map/all_gather | solution.py:30
  1289.9 8.0 broadcast_multiply_fusion.1
  1297.9 56.1 %all-gather.23.cloned.1.call-done = f32[3072,768]{1,0:T(8,128)} async-done(((f32[768,768]{1,0:T(8,128)}), f32[3072,768]{1,0:T(8,128)}) %all-gather.23.cloned.1.call-update) | async-done | bytes 9437200 | tf_op jit(solution)/shard_map/all_gather | solution.py:30
  1354.0 8.0 broadcast_multiply_fusion
  1362.0 56.1 %all-gather.19.cloned.1.call-done = f32[768,3072]{1,0:T(8,128)} async-done(((f32[192,3072]{1,0:T(8,128)}), f32[768,3072]{1,0:T(8,128)}) %all-gather.19.cloned.1.call-update) | async-done | bytes 9437200 | tf_op jit(solution)/shard_map/all_gather | solution.py:30
  1418.1 9.1 broadcast_multiply_fusion.2
  (10 shorter events, 0.1 us)
Async XLA Ops:
  7.2 632.2 %reduce-scatter.29.cloned.1.call-start = ((), (), s32[]{:S(2)}) async-start(), calls=%async_computation.22 | async-start | bytes 11796480
  7.2 47.2 %copy-start.1 = (bf16[3072,768]{1,0:T(8,128)(2,1)S(1)}, bf16[3072,768]{1,0:T(8,128)(2,1)}, u32[]{:S(2)}) copy-start(bf16[3072,768]{1,0:T(8,128)(2,1)} %param.9) | copy-start | bytes 14155780
  124.1 47.5 %copy-start = (bf16[3072,768]{1,0:T(8,128)(2,1)S(1)}, bf16[3072,768]{1,0:T(8,128)(2,1)}, u32[]{:S(2)}) copy-start(bf16[3072,768]{1,0:T(8,128)(2,1)} %param.11) | copy-start | bytes 14155780
  312.7 327.2 %reduce-scatter.25.cloned.1.call-start = ((), (), s32[]{:S(2)}) async-start(), calls=%async_computation.20 | async-start | bytes 11796480
  512.5 152.8 %reduce-scatter.21.cloned.1.call-start = ((), (), s32[]{:S(2)}) async-start(), calls=%async_computation.16 | async-start | bytes 11796480 | tf_op jit(solution)/shard_map/reduce_scatter | solution.py:26
  575.8 165.9 %reduce-scatter.17.cloned.1.call-start = ((), (), s32[]{:S(2)}) async-start(), calls=%async_computation.10 | async-start | bytes 11796480 | tf_op jit(solution)/shard_map/reduce_scatter | solution.py:26
  639.3 137.4 %reduce-scatter.31.cloned.1.call-start = ((), (), s32[]{:S(2)}) async-start(), calls=%async_computation.23 | async-start | bytes 3538944
  639.9 171.7 %reduce-scatter.27.cloned.1.call-start = ((), (), s32[]{:S(2)}) async-start(), calls=%async_computation.21 | async-start | bytes 3538944
  640.4 206.2 %reduce-scatter.23.cloned.1.call-start = ((), (), s32[]{:S(2)}) async-start(), calls=%async_computation.17 | async-start | bytes 3538944 | tf_op jit(solution)/shard_map/reduce_scatter | solution.py:27
  665.3 216.4 %reduce-scatter.19.cloned.1.call-start = ((), (), s32[]{:S(2)}) async-start(), calls=%async_computation.11 | async-start | bytes 3538944 | tf_op jit(solution)/shard_map/reduce_scatter | solution.py:27
  741.7 275.6 %all-reduce.3.cloned.1.call-start = ((), (), s32[]{:S(2)}) async-start(), calls=%async_computation.24 | async-start | bytes 11010048 | tf_op jit(solution)/shard_map/psum | solution.py:28
  881.7 172.7 %all-gather.9.cloned.1.call-start = ((), (), s32[]{:S(2)}) async-start(), calls=%async_computation.8 | async-start | bytes 3538944 | tf_op jit(solution)/shard_map/all_gather | solution.py:29
  1020.2 69.8 %all-gather.13.cloned.1.call-start = ((), (), s32[]{:S(2)}) async-start(), calls=%async_computation.12 | async-start | bytes 3538944 | tf_op jit(solution)/shard_map/all_gather | solution.py:29
  1020.9 104.5 %all-gather.21.cloned.1.call-start = ((), (), s32[]{:S(2)}) async-start(), calls=%async_computation.18 | async-start | bytes 3538944 | tf_op jit(solution)/shard_map/all_gather | solution.py:29
  1021.5 140.1 %all-gather.17.cloned.1.call-start = ((), (), s32[]{:S(2)}) async-start(), calls=%async_computation.14 | async-start | bytes 3538944 | tf_op jit(solution)/shard_map/all_gather | solution.py:29
  1024.5 201.3 %all-gather.11.cloned.1.call-start = ((), (), s32[]{:S(2)}) async-start(), calls=%async_computation.9 | async-start | bytes 11796480 | tf_op jit(solution)/shard_map/all_gather | solution.py:30
  1054.4 235.4 %all-gather.15.cloned.1.call-start = ((), (), s32[]{:S(2)}) async-start(), calls=%async_computation.13 | async-start | bytes 11796480 | tf_op jit(solution)/shard_map/all_gather | solution.py:30
  1090.0 263.9 %all-gather.23.cloned.1.call-start = ((), (), s32[]{:S(2)}) async-start(), calls=%async_computation.19 | async-start | bytes 11796480 | tf_op jit(solution)/shard_map/all_gather | solution.py:30
  1125.5 292.6 %all-gather.19.cloned.1.call-start = ((), (), s32[]{:S(2)}) async-start(), calls=%async_computation.15 | async-start | bytes 11796480 | tf_op jit(solution)/shard_map/all_gather | solution.py:30
Sparse Core Ops, SparseCore 0:
  312.8 76.1 reduce-scatter.28
  512.6 76.1 reduce-scatter.24
  591.9 73.3 reduce-scatter.20
  668.3 73.3 reduce-scatter.16
  743.8 32.8 reduce-scatter.30
  778.7 32.7 reduce-scatter.26
  813.8 32.7 reduce-scatter.22
  848.9 32.7 reduce-scatter.18
  885.0 132.2 all-reduce.2
  1020.3 34.0 all-gather.8
  1055.9 34.0 all-gather.12
  1091.4 34.0 all-gather.20
  1127.6 34.0 all-gather.16
  1163.1 62.6 all-gather.10
  1227.2 62.6 all-gather.14
  1291.3 62.6 all-gather.22
  1355.4 62.6 all-gather.18
where the time goes:
time: 1440 us; the launch traced here: 1430 us
  waiting for transfers between devices  741 us (51%)
  matrix products  622 us (43%)
  other arithmetic  34.3 us (2%)
  local copies, waits for them, and re-layouts  21.1 us (1%)
  between operations  14.5 us (1%)
    all_gather x4, waiting for transfers between devices, reduce_grad(): reduced = lax.all_gather(reduced, 'xc', axis=0, tiled=True)  231 us
    all_gather x4, waiting for transfers between devices, reduce_grad(): reduced = lax.all_gather(reduced, 'y', axis=0, tiled=True)  137 us
    psum x1, waiting for transfers between devices, reduce_grad(): reduced = lax.psum(reduced, 'z')  136 us
    reduce_scatter x2, waiting for transfers between devices, reduce_grad(): lax.psum_scatter(local_grad, 'xc', scatter_dimension=0, tiled=True)  101 us
    dot_general x1, matrix products, device_step(): jnp.einsum('nd,fd->nf', d_h2, w_two, preferred_element_type=jnp.float32)  94 us
    dot_general x1, matrix products, device_step(): jnp.einsum('nd,fd->nf', g_loc, w_four, preferred_element_type=jnp.float32)  92.7 us
    dot_general x1, matrix products, device_step(): jnp.dot(h_one, w_two, preferred_element_type=jnp.float32)  69.6 us
    unnamed x21, waiting for transfers between devices  69.4 us
  transfers between devices with their start and end apart: 17, of which 15 were waited for; matrix products, arithmetic and copies ran while one was open for 25% of the time, Pallas kernels for 0%

commit v1 on v0

v1 whole, which is shorter than its diff:
```python
import functools
import math
import jax
import jax.numpy as jnp
from jax import lax
from jax.experimental import pallas as pl
from jax.experimental.pallas import tpu as pltpu
from jax.sharding import PartitionSpec as P

GELU_SCALE = math.sqrt(2.0 / math.pi)
GELU_CUBIC = 0.044715
F32 = jnp.float32
BF16 = jnp.bfloat16
MESH = pl.DeviceIdType.MESH
COLORS = 3
CHUNKS = 4
TILE = 512
RS_STEPS = (0, 2, 7, 11, 13)
AG_STEPS = (0, 2, 6, 11, 13, 15)
MID_RS_STEPS = (0, 2, 6, 8, 9)
MID_AG_STEPS = (0, 2, 4, 7, 9, 15)
MID_LAST_STEPS = (9, 11, 12, 15)


def dot(a, b):
    return jnp.dot(a, b, preferred_element_type=F32)


def dot_rows(a, b):
    return lax.dot_general(a, b, (((0,), (0,)), ((), ())), preferred_element_type=F32)


def gelu_tanh(pre_act, square):
    return jnp.tanh(pre_act * (GELU_SCALE + (GELU_SCALE * GELU_CUBIC) * square))


def gelu_value(pre_act):
    return (0.5 * pre_act) * (1.0 + gelu_tanh(pre_act, pre_act * pre_act))


def gelu_both(pre_act):
    square = pre_act * pre_act
    tanh_val = gelu_tanh(pre_act, square)
    half = 0.5 * pre_act
    value = half * (1.0 + tanh_val)
    slope = (0.5 + 0.5 * tanh_val) + (half * (1.0 - tanh_val * tanh_val)) * (GELU_SCALE + (3.0 * GELU_SCALE * GELU_CUBIC) * square)
    return value, slope


class Reducer:
    def __init__(self, n_dev, q, full, b0, b1, b2, b3, rs_send, rs_recv, ag_send, ag_recv, out_sem, carry_sem):
        self.q, self.full, self.bufs, self.n_dev = q, full, (b0, b1, b2, b3), n_dev
        self.out_sem, self.carry_sem = out_sem, carry_sem
        self.rs_send, self.rs_recv, self.ag_send, self.ag_recv = rs_send, rs_recv, ag_send, ag_recv
        self.side = q.shape[2]
        z, y, xc = lax.axis_index("z"), lax.axis_index("y"), lax.axis_index("xc")
        x, core = xc // 2, xc % 2
        self.core = core
        self.bits = (x, y, z)
        self.peers = (
            (z, y, (1 - x) * 2 + core),
            (z, 1 - y, xc),
            (1 - z, y, xc),
        )
        self.other_core = (z, y, x * 2 + (1 - core))

    def barrier(self):
        sem = pltpu.get_barrier_semaphore()
        for peer in self.peers + (self.other_core,):
            pl.semaphore_signal(sem, inc=1, device_id=peer, device_id_type=MESH)
        pl.semaphore_wait(sem, 4)

    def rows(self, color, depth):
        count = self.side // COLORS
        start = self.core * self.side + color * count
        for level in range(depth):
            count //= 2
            start = start + self.bits[(color + level) % 3] * count
        return start, count

    def part(self, ref, par, start, count):
        return ref.at[par, pl.ds(pl.multiple_of(start, 32), count), :]

    def rs_copy(self, stage, color, chunk):
        par = chunk % 2
        if stage == 0:
            count = self.side // COLORS
            start = (1 - self.core) * self.side + color * count
            peer = self.other_core
        else:
            axis = (color + stage - 1) % 3
            start, count = self.rows(color, stage - 1)
            count //= 2
            start = start + (1 - self.bits[axis]) * count
            peer = self.peers[axis]
        return pltpu.make_async_remote_copy(
            src_ref=self.part(self.q, par, start, count),
            dst_ref=self.bufs[stage].at[par, color],
            send_sem=self.rs_send.at[stage, color],
            recv_sem=self.rs_recv.at[par, stage, color],
            device_id=peer,
            device_id_type=MESH,
        )

    def rs(self, stage, chunk):
        par = chunk % 2
        for color in range(COLORS):
            if stage > 0:
                self.rs_copy(stage - 1, color, chunk).wait()
                start, count = self.rows(color, stage - 1)
                part = self.part(self.q, par, start, count)
                total = part[...] + self.bufs[stage - 1][par, color]
                if stage == 4:
                    self.part(self.full, par, start, count)[...] = total * (1.0 / self.n_dev)
                else:
                    part[...] = total
            if stage < 4:
                self.rs_copy(stage, color, chunk).start()

    def ag_copy(self, stage, color, chunk):
        par = chunk % 2
        start, count = self.rows(color, 3 - stage)
        peer = self.other_core if stage == 3 else self.peers[(color + 2 - stage) % 3]
        part = self.part(self.full, par, start, count)
        return pltpu.make_async_remote_copy(
            src_ref=part,
            dst_ref=part,
            send_sem=self.ag_send.at[stage, color],
            recv_sem=self.ag_recv.at[par, stage, color],
            device_id=peer,
            device_id_type=MESH,
        )

    def ag(self, stage, chunk):
        for color in range(COLORS):
            if stage > 0:
                self.ag_copy(stage - 1, color, chunk).wait()
            if stage < 4:
                self.ag_copy(stage, color, chunk).start()


    def out_copies(self, chunk, index, rows_out, cols_out):
        par, side = chunk % 2, self.side
        span = pl.ds(pl.multiple_of(index * side, side), side)
        return (
            pltpu.make_async_copy(self.full.at[par, pl.ds(0, side), :], rows_out.at[span, :], self.out_sem.at[par, 0]),
            pltpu.make_async_copy(self.full.at[par, pl.ds(side, side), :], cols_out.at[:, span], self.out_sem.at[par, 1]),
        )

    def carry_copies(self, chunk, partial, pieces, load):
        pairs = [(self.q.at[chunk % 2], partial)]
        for color in range(COLORS):
            start, count = self.rows(color, 3)
            pairs.append((self.part(self.full, (chunk - 1) % 2, start, count), pieces.at[color]))
        return [
            pltpu.make_async_copy(far if load else near, near if load else far, self.carry_sem.at[k])
            for k, (near, far) in enumerate(pairs)
        ]


def run(copies):
    for copy in copies:
        copy.start()
    for copy in copies:
        copy.wait()


def chunk_events(red, j, r, rows_out, cols_out):
    @pl.when(jnp.logical_and(j == 0, r == 0))
    def _():
        red.barrier()

    for stage, step in enumerate(RS_STEPS):
        @pl.when(jnp.logical_and(j >= 1, r == step))
        def _():
            red.rs(stage, j - 1)

    for stage, step in enumerate(AG_STEPS):
        @pl.when(jnp.logical_and(j >= 2, r == step))
        def _():
            if stage < 5:
                red.ag(stage, j - 2)
            if stage >= 4:
                for copy in red.out_copies(j - 2, j - 2, rows_out, cols_out):
                    copy.start() if stage == 4 else copy.wait()


def forward_kernel(x_ref, w1_ref, w2_ref, a1_ref, h2_ref):
    width = w1_ref.shape[1] // CHUNKS
    x = x_ref[...]
    total = x.astype(F32)
    for c in range(CHUNKS):
        cols = slice(c * width, (c + 1) * width)
        a = dot(x, w1_ref[:, cols]).astype(BF16)
        a1_ref[:, cols] = a
        total = total + dot(gelu_value(a.astype(F32)).astype(BF16), w2_ref[cols, :])
    h2_ref[...] = total.astype(BF16)


def upper_kernel(n_dev, steps, h2_ref, g_ref, w3_ref, w4t_ref, da3_ref, rows_out, cols_out, partial_out, pieces_out, *refs):
    j, r = pl.program_id(0), pl.program_id(1)
    red = Reducer(n_dev, *refs)
    q, side, slot = red.q, red.side, j % 2
    chunk_events(red, j, r, rows_out, cols_out)

    @pl.when(r == 0)
    def _():
        q[slot] = jnp.zeros(q.shape[1:], F32)

    h2, g = h2_ref[...], g_ref[...]
    a3 = dot(h2, w3_ref[...]).astype(BF16)
    back = dot(g, w4t_ref[...])
    value, slope = gelu_both(a3.astype(F32))
    h3 = value.astype(BF16)
    da3 = (back * slope).astype(BF16)
    da3_ref[...] = da3
    q[slot, 0:side, :] += dot_rows(h3, g)
    q[slot, side:2 * side, :] += dot_rows(h2, da3)

    @pl.when(jnp.logical_and(j == CHUNKS - 1, r == steps - 1))
    def _():
        run(red.carry_copies(CHUNKS - 1, partial_out, pieces_out, False))


def middle_kernel(n_dev, steps, da3_ref, w3_ref, g_ref, partial_ref, pieces_ref, dh2_ref, rows_out, cols_out, *refs):
    r = pl.program_id(0)
    red = Reducer(n_dev, *refs)
    last = CHUNKS - 1

    @pl.when(r == 0)
    def _():
        run(red.carry_copies(last, partial_ref, pieces_ref, True))
        red.barrier()

    for stage, step in enumerate(MID_RS_STEPS):
        @pl.when(r == step)
        def _():
            red.rs(stage, last)

    for stage, step in enumerate(MID_AG_STEPS):
        @pl.when(r == step)
        def _():
            if stage < 5:
                red.ag(stage, last - 1)
            if stage >= 4:
                for copy in red.out_copies(last - 1, 0, rows_out, cols_out):
                    copy.start() if stage == 4 else copy.wait()

    for stage, step in enumerate(MID_LAST_STEPS):
        @pl.when(r == step)
        def _():
            red.ag(stage, last)

    back = lax.dot_general(da3_ref[...], w3_ref[...], (((1,), (1,)), ((), ())), preferred_element_type=F32)
    dh2_ref[...] = (back + g_ref[...].astype(F32)).astype(BF16)

    @pl.when(r == steps - 1)
    def _():
        red.ag(4, last)
        run(red.out_copies(last, 1, rows_out, cols_out))


def lower_kernel(n_dev, steps, x_ref, dh2_ref, a1_ref, w2t_ref, rows_out, cols_out, *refs):
    j, r = pl.program_id(0), pl.program_id(1)
    red = Reducer(n_dev, *refs)
    q, side, slot = red.q, red.side, j % 2
    chunk_events(red, j, r, rows_out, cols_out)

    @pl.when(r == 0)
    def _():
        q[slot] = jnp.zeros(q.shape[1:], F32)

    x, dh2 = x_ref[...], dh2_ref[...]
    back = dot(dh2, w2t_ref[...])
    value, slope = gelu_both(a1_ref[...].astype(F32))
    h1 = value.astype(BF16)
    da1 = (back * slope).astype(BF16)
    q[slot, 0:side, :] += dot_rows(h1, dh2)
    q[slot, side:2 * side, :] += dot_rows(x, da1)

    @pl.when(jnp.logical_and(j == CHUNKS - 1, r == steps - 1))
    def _():
        last = CHUNKS - 1
        for stage in range(5):
            red.rs(stage, last)
            red.ag(stage, last - 1)
        first = red.out_copies(last - 1, last - 1, rows_out, cols_out)
        for copy in first:
            copy.start()
        for stage in range(5):
            red.ag(stage, last)
        run(red.out_copies(last, last, rows_out, cols_out))
        for copy in first:
            copy.wait()


def scratch(side):
    part = side // COLORS
    return [
        pltpu.VMEM((2, 2 * side, side), F32),
        pltpu.VMEM((2, 2 * side, side), F32),
        pltpu.VMEM((2, COLORS, part, side), F32),
        pltpu.VMEM((2, COLORS, part // 2, side), F32),
        pltpu.VMEM((2, COLORS, part // 4, side), F32),
        pltpu.VMEM((2, COLORS, part // 8, side), F32),
        pltpu.SemaphoreType.DMA((4, COLORS)),
        pltpu.SemaphoreType.DMA((2, 4, COLORS)),
        pltpu.SemaphoreType.DMA((4, COLORS)),
        pltpu.SemaphoreType.DMA((2, 4, COLORS)),
        pltpu.SemaphoreType.DMA((2, 2)),
        pltpu.SemaphoreType.DMA((4,)),
    ]


def solution(mesh):
    n_dev = math.prod(mesh.shape.values())
    batch_spec = P(("z", "y", "xc"), None)
    whole_spec = P(None, None)

    def device_step(x, g, w_one, w_two, w_three, w_four):
        n, d = x.shape
        ff = w_one.shape[1]
        steps = n // TILE
        side = ff // CHUNKS
        any_spec = pl.BlockSpec(memory_space=pl.ANY)

        def params(collective=None):
            if collective is None:
                return pltpu.CompilerParams(vmem_limit_bytes=60 * 2**20)
            return pltpu.CompilerParams(vmem_limit_bytes=62 * 2**20, collective_id=collective, has_side_effects=True)

        a_one, h_two = pl.pallas_call(
            forward_kernel,
            grid=(steps,),
            in_specs=[
                pl.BlockSpec((TILE, d), lambda r: (r, 0)),
                pl.BlockSpec((d, ff), lambda r: (0, 0)),
                pl.BlockSpec((ff, d), lambda r: (0, 0)),
            ],
            out_specs=[pl.BlockSpec((TILE, ff), lambda r: (r, 0)), pl.BlockSpec((TILE, d), lambda r: (r, 0))],
            out_shape=[jax.ShapeDtypeStruct((n, ff), BF16), jax.ShapeDtypeStruct((n, d), BF16)],
            compiler_params=params(),
            name="forward",
        )(x, w_one, w_two)

        tile_spec = pl.BlockSpec((TILE, d), lambda j, r: (r, 0))
        col_spec = pl.BlockSpec((TILE, side), lambda j, r: (r, j))
        w_spec = pl.BlockSpec((d, side), lambda j, r: (0, j))

        half_rows = jax.ShapeDtypeStruct((2 * side, d), F32)
        half_cols = jax.ShapeDtypeStruct((d, 2 * side), F32)

        d_a3, w4_a, w3_a, partial, pieces = pl.pallas_call(
            functools.partial(upper_kernel, n_dev, steps),
            grid=(CHUNKS, steps),
            in_specs=[tile_spec, tile_spec, w_spec, w_spec],
            out_specs=[col_spec] + [any_spec] * 4,
            out_shape=[
                jax.ShapeDtypeStruct((n, ff), BF16),
                half_rows,
                half_cols,
                jax.ShapeDtypeStruct((2 * side, side), F32),
                jax.ShapeDtypeStruct((COLORS, side // COLORS // 8, side), F32),
            ],
            scratch_shapes=scratch(side),
            compiler_params=params(0),
            name="upper",
        )(h_two, g, w_three, w_four.T)

        d_h2, w4_b, w3_b = pl.pallas_call(
            functools.partial(middle_kernel, n_dev, steps),
            grid=(steps,),
            in_specs=[
                pl.BlockSpec((TILE, ff), lambda r: (r, 0)),
                pl.BlockSpec((d, ff), lambda r: (0, 0)),
                pl.BlockSpec((TILE, d), lambda r: (r, 0)),
                any_spec,
                any_spec,
            ],
            out_specs=[pl.BlockSpec((TILE, d), lambda r: (r, 0)), any_spec, any_spec],
            out_shape=[jax.ShapeDtypeStruct((n, d), BF16), half_rows, half_cols],
            scratch_shapes=scratch(side),
            compiler_params=params(1),
            name="middle",
        )(d_a3, w_three, g, partial, pieces)

        grad_w2, grad_w1 = pl.pallas_call(
            functools.partial(lower_kernel, n_dev, steps),
            grid=(CHUNKS, steps),
            in_specs=[tile_spec, tile_spec, col_spec, w_spec],
            out_specs=[any_spec] * 2,
            out_shape=[jax.ShapeDtypeStruct((ff, d), F32), jax.ShapeDtypeStruct((d, ff), F32)],
            scratch_shapes=scratch(side),
            compiler_params=params(2),
            name="lower",
        )(x, d_h2, a_one, w_two.T)

        grad_w4 = jnp.concatenate([w4_a, w4_b], axis=0)
        grad_w3 = jnp.concatenate([w3_a, w3_b], axis=1)
        return grad_w1, grad_w2, grad_w3, grad_w4

    return jax.shard_map(
        device_step,
        mesh=mesh,
        in_specs=(batch_spec, batch_spec, whole_spec, whole_spec, whole_spec, whole_spec),
        out_specs=(whole_spec, whole_spec, whole_spec, whole_spec),
        check_vma=False,
    )
```

time: 1440 us -> 679 us (0.47)
  waiting for transfers between devices: 741 us -> 0 us
  Pallas kernels: 0 us -> 639 us
  matrix products: 622 us -> 0 us
  other arithmetic: 34.3 us -> 13.4 us
    pallas_call x0 -> x4, Pallas kernels: none -> 639 us  [the longest x1 251 us: device_step(): pl.pallas_call(functools.partial(lower_kernel, n_dev, steps), grid=(CHUNK...]
    dot_general x9 -> x0, matrix products: 574 us -> none  [the longest x1 94 us: device_step(): jnp.einsum('nd,fd->nf', d_h2, w_two, preferred_element_type=jnp.float32)]
    all_gather x8 -> x0, waiting for transfers between devices: 368 us -> none  [the longest x4 231 us: reduce_grad(): reduced = lax.all_gather(reduced, 'xc', axis=0, tiled=True)]
    reduce_scatter x4 -> x0, waiting for transfers between devices: 168 us -> none  [the longest x2 101 us: reduce_grad(): lax.psum_scatter(local_grad, 'xc', scatter_dimension=0, tiled=True)]
    psum x1 -> x0, waiting for transfers between devices: 136 us -> none  [reduce_grad(): reduced = lax.psum(reduced, 'z')]
    unnamed x21 -> x0, waiting for transfers between devices: 69.4 us -> none
    unnamed x1 -> x0, matrix products: 48.3 us -> none
    div x4 -> x0, other arithmetic: 34.3 us -> none  [reduce_grad(): return reduced / n_dev]
  transfers between devices with their start and end apart: 17 -> 0, of which waited for: 15 -> 0; matrix products, arithmetic and copies ran while one was open for 25% -> 0% of each run, Pallas kernels for 0% -> 0%
where the time goes in v1:
time: 679 us; the launch traced here: 678 us
  Pallas kernels  639 us (94%)
  local copies, waits for them, and re-layouts  25.8 us (4%)
  other arithmetic  13.4 us (2%)
    pallas_call x1, Pallas kernels, device_step(): pl.pallas_call(functools.partial(lower_kernel, n_dev, steps), grid=(CHUNK...  251 us
    pallas_call x1, Pallas kernels, device_step(): pl.pallas_call(functools.partial(upper_kernel, n_dev, steps), grid=(CHUNK...  220 us
    pallas_call x1, Pallas kernels, device_step(): pl.pallas_call(forward_kernel, grid=(steps,), in_specs=[pl.BlockSpec((TIL...  92.1 us
    pallas_call x1, Pallas kernels, device_step(): pl.pallas_call(functools.partial(middle_kernel, n_dev, steps), grid=(step...  75.6 us
    unnamed x10, local copies, waits for them, and re-layouts  25.8 us

profile of v1, /device:TPU:0, one launch (start us, length us, event | category | flops | bytes accessed | tf_op | source)
XLA Modules:
  0.0 678.5 jit_solution(17471910145155363540)
XLA Ops:
  0.6 92.1 %forward.1 = (bf16[8192,3072]{1,0:T(8,128)(2,1)}, bf16[8192,768]{1,0:T(8,128)(2,1)}) custom-call(bf16[8192,768]{1,0:T(8,128)(2,1)} %x_ref.3, bf16[768,3072]{1,0:T(8,128)(2,1)} %w1_ref.1, bf16[3072,768]{1,0:T(8,128)(2,1)} %w2_ref.1), custom_call_target="tpu_custom_call" | custom-call | tf_op jit(solution)/shard_map/forward/pallas_call | solution.py:332
  92.7 6.6 copy.10
  99.4 219.6 %upper.1 = (bf16[8192,3072]{1,0:T(8,128)(2,1)}, f32[1536,768]{1,0:T(8,128)}, f32[768,1536]{1,0:T(8,128)}, f32[1536,768]{1,0:T(8,128)}, f32[3,32,768]{2,1,0:T(8,128)}) custom-call(bf16[8192,768]{1,0:T(8,128)(2,1)} %get-tuple-element.16.h2_ref, bf16[8192,768]{1,0:T(8,128)(2,1)} %g_ref.3, bf16[768,3072]{1,0:T(8,128)(2,1)} %w3_ref.3, bf16[768,3072]{1,0:T(8,128)(2,1)} %bitcast.3), custom_call_target="tpu_custom_call" | custom-call | tf_op jit(solution)/shard_map/upper/pallas_call | solution.py:353
  319.0 75.6 %middle.1 = (bf16[8192,768]{1,0:T(8,128)(2,1)}, f32[1536,768]{1,0:T(8,128)}, f32[768,1536]{1,0:T(8,128)}) custom-call(bf16[8192,3072]{1,0:T(8,128)(2,1)} %get-tuple-element.17.da3_ref, bf16[768,3072]{1,0:T(8,128)(2,1)} %w3_ref.3, bf16[8192,768]{1,0:T(8,128)(2,1)} %g_ref.3, f32[1536,768]{1,0:T(8,128)} %get-tuple-element.18.partial_ref, ...), custom_call_target="tpu_custom_call" | custom-call | tf_op jit(solution)/shard_map/middle/pallas_call | solution.py:370
  394.6 0.0 copy-start.1
  394.6 0.0 copy-start.2
  394.6 8.8 %pad_maximum_fusion.1 = f32[3072,768]{1,0:T(8,128)} fusion(f32[1536,768]{1,0:T(8,128)} %get-tuple-element.27, f32[1536,768]{1,0:T(8,128)} %get-tuple-element.26), kind=kLoop, calls=%fused_computation.1 | loop fusion | flops 2359296 | bytes 18874368 | tf_op jit(solution)/shard_map/concatenate | solution.py:398
  403.5 0.0 copy-done.1
  403.5 0.0 copy-done.2
  403.5 4.6 pad_maximum_fusion
  408.1 6.6 copy.11
  414.7 251.3 %lower.1 = (f32[3072,768]{1,0:T(8,128)}, f32[768,3072]{1,0:T(8,128)}) custom-call(bf16[8192,768]{1,0:T(8,128)(2,1)} %x_ref.3, bf16[8192,768]{1,0:T(8,128)(2,1)} %get-tuple-element.20.dh2_ref, bf16[8192,3072]{1,0:T(8,128)(2,1)} %get-tuple-element.21.a1_ref, bf16[768,3072]{1,0:T(8,128)(2,1)} %bitcast.2), custom_call_target="tpu_custom_call" | custom-call | tf_op jit(solution)/shard_map/lower/pallas_call | solution.py:387
  666.0 0.0 copy-start
  666.0 8.8 %copy.14 = f32[768,3072]{1,0:T(8,128)} copy(f32[768,3072]{1,0:T(8,128)} %get-tuple-element.32) | data formatting | bytes 18874368
  674.7 0.0 copy-done
  674.8 3.7 copy.15
Async XLA Ops:
  394.6 8.8 %copy-start.1 = (f32[768,1536]{1,0:T(8,128)S(1)}, f32[768,1536]{1,0:T(8,128)}, u32[]{:S(2)}) copy-start(f32[768,1536]{1,0:T(8,128)} %get-tuple-element.24) | copy-start | bytes 14155780
  394.6 8.9 %copy-start.2 = (f32[768,1536]{1,0:T(8,128)S(1)}, f32[768,1536]{1,0:T(8,128)}, u32[]{:S(2)}) copy-start(f32[768,1536]{1,0:T(8,128)} %get-tuple-element.25) | copy-start | bytes 14155780
  666.0 8.8 %copy-start = (f32[3072,768]{1,0:T(8,128)S(1)}, f32[3072,768]{1,0:T(8,128)}, u32[]{:S(2)}) copy-start(f32[3072,768]{1,0:T(8,128)} %get-tuple-element.33) | copy-start | bytes 28311556

commit v2 on v1

--- a/solution.py
+++ b/solution.py
@@ -15,11 +15,14 @@
 COLORS = 3
 CHUNKS = 4
 TILE = 512
-RS_STEPS = (0, 2, 7, 11, 13)
-AG_STEPS = (0, 2, 6, 11, 13, 15)
-MID_RS_STEPS = (0, 2, 6, 8, 9)
-MID_AG_STEPS = (0, 2, 4, 7, 9, 15)
-MID_LAST_STEPS = (9, 11, 12, 15)
+UP_TILE = 1024
+LOW_TILE = 1024
+TRANS_B = True
+RS_STEPS = (0, 1, 4, 7, 0)
+AG_STEPS = (0, 1, 4, 7, 1, 3)
+MID_RS_STEPS = (0, 2, 6, 9, 10)
+MID_AG_STEPS = (0, 2, 6, 10, 12, 15)
+MID_LAST_STEPS = (10, 12, 14, 15)
 
 
 def dot(a, b):
@@ -28,6 +31,10 @@
 
 def dot_rows(a, b):
     return lax.dot_general(a, b, (((0,), (0,)), ((), ())), preferred_element_type=F32)
+
+
+def dot_back(a, w):
+    return lax.dot_general(a, w, (((1,), (1 if TRANS_B else 0,)), ((), ())), preferred_element_type=F32)
 
 
 def gelu_tanh(pre_act, square):
@@ -170,19 +177,29 @@
     def _():
         red.barrier()
 
-    for stage, step in enumerate(RS_STEPS):
-        @pl.when(jnp.logical_and(j >= 1, r == step))
+    @pl.when(jnp.logical_and(j >= 2, r == RS_STEPS[4]))
+    def _():
+        red.rs(4, j - 2)
+
+    for stage in range(4):
+        @pl.when(jnp.logical_and(j >= 1, r == RS_STEPS[stage]))
         def _():
             red.rs(stage, j - 1)
 
-    for stage, step in enumerate(AG_STEPS):
-        @pl.when(jnp.logical_and(j >= 2, r == step))
+        @pl.when(jnp.logical_and(j >= 2, r == AG_STEPS[stage]))
         def _():
-            if stage < 5:
-                red.ag(stage, j - 2)
-            if stage >= 4:
-                for copy in red.out_copies(j - 2, j - 2, rows_out, cols_out):
-                    copy.start() if stage == 4 else copy.wait()
+            red.ag(stage, j - 2)
+
+    @pl.when(jnp.logical_and(j >= 3, r == AG_STEPS[4]))
+    def _():
+        red.ag(4, j - 3)
+        for copy in red.out_copies(j - 3, j - 3, rows_out, cols_out):
+            copy.start()
+
+    @pl.when(jnp.logical_and(j >= 3, r == AG_STEPS[5]))
+    def _():
+        for copy in red.out_copies(j - 3, j - 3, rows_out, cols_out):
+            copy.wait()
 
 
 def forward_kernel(x_ref, w1_ref, w2_ref, a1_ref, h2_ref):
@@ -197,7 +214,7 @@
     h2_ref[...] = total.astype(BF16)
 
 
-def upper_kernel(n_dev, steps, h2_ref, g_ref, w3_ref, w4t_ref, da3_ref, rows_out, cols_out, partial_out, pieces_out, *refs):
+def upper_kernel(n_dev, steps, h2_ref, g_ref, w3_ref, w4t_ref, da3_ref, rows_out, cols_out, partial_out, pieces_out, h3_buf, *refs):
     j, r = pl.program_id(0), pl.program_id(1)
     red = Reducer(n_dev, *refs)
     q, side, slot = red.q, red.side, j % 2
@@ -207,19 +224,22 @@
     def _():
         q[slot] = jnp.zeros(q.shape[1:], F32)
 
-    h2, g = h2_ref[...], g_ref[...]
-    a3 = dot(h2, w3_ref[...]).astype(BF16)
-    back = dot(g, w4t_ref[...])
-    value, slope = gelu_both(a3.astype(F32))
-    h3 = value.astype(BF16)
-    da3 = (back * slope).astype(BF16)
-    da3_ref[...] = da3
-    q[slot, 0:side, :] += dot_rows(h3, g)
-    q[slot, side:2 * side, :] += dot_rows(h2, da3)
+    for start in range(0, h2_ref.shape[0], TILE):
+        span = slice(start, start + TILE)
+        a3 = dot(h2_ref[span, :], w3_ref[...]).astype(BF16)
+        back = dot_back(g_ref[span, :], w4t_ref[...])
+        value, slope = gelu_both(a3.astype(F32))
+        h3_buf[span, :] = value.astype(BF16)
+        da3_ref[span, :] = (back * slope).astype(BF16)
+    q[slot, 0:side, :] += dot_rows(h3_buf[...], g_ref[...])
+    q[slot, side:2 * side, :] += dot_rows(h2_ref[...], da3_ref[...])
 
     @pl.when(jnp.logical_and(j == CHUNKS - 1, r == steps - 1))
     def _():
-        run(red.carry_copies(CHUNKS - 1, partial_out, pieces_out, False))
+        last = CHUNKS - 1
+        red.rs(4, last - 1)
+        red.ag(4, last - 2)
+        run(list(red.out_copies(last - 2, last - 2, rows_out, cols_out)) + red.carry_copies(last, partial_out, pieces_out, False))
 
 
 def middle_kernel(n_dev, steps, da3_ref, w3_ref, g_ref, partial_ref, pieces_ref, dh2_ref, rows_out, cols_out, *refs):
@@ -260,7 +280,7 @@
         run(red.out_copies(last, 1, rows_out, cols_out))
 
 
-def lower_kernel(n_dev, steps, x_ref, dh2_ref, a1_ref, w2t_ref, rows_out, cols_out, *refs):
+def lower_kernel(n_dev, steps, x_ref, dh2_ref, a1_ref, w2t_ref, rows_out, cols_out, h1_buf, da1_buf, *refs):
     j, r = pl.program_id(0), pl.program_id(1)
     red = Reducer(n_dev, *refs)
     q, side, slot = red.q, red.side, j % 2
@@ -270,27 +290,40 @@
     def _():
         q[slot] = jnp.zeros(q.shape[1:], F32)
 
-    x, dh2 = x_ref[...], dh2_ref[...]
-    back = dot(dh2, w2t_ref[...])
-    value, slope = gelu_both(a1_ref[...].astype(F32))
-    h1 = value.astype(BF16)
-    da1 = (back * slope).astype(BF16)
-    q[slot, 0:side, :] += dot_rows(h1, dh2)
-    q[slot, side:2 * side, :] += dot_rows(x, da1)
+    for start in range(0, x_ref.shape[0], TILE):
+        span = slice(start, start + TILE)
+        back = dot_back(dh2_ref[span, :], w2t_ref[...])
+        value, slope = gelu_both(a1_ref[span, :].astype(F32))
+        h1_buf[span, :] = value.astype(BF16)
+        da1_buf[span, :] = (back * slope).astype(BF16)
+    q[slot, 0:side, :] += dot_rows(h1_buf[...], dh2_ref[...])
+    q[slot, side:2 * side, :] += dot_rows(x_ref[...], da1_buf[...])
 
     @pl.when(jnp.logical_and(j == CHUNKS - 1, r == steps - 1))
     def _():
         last = CHUNKS - 1
-        for stage in range(5):
+        outs = [red.out_copies(chunk, chunk, rows_out, cols_out) for chunk in (last - 2, last - 1, last)]
+        red.rs(0, last)
+        red.rs(4, last - 1)
+        red.ag(0, last - 1)
+        red.ag(4, last - 2)
+        for copy in outs[0]:
+            copy.start()
+        for stage in range(1, 4):
             red.rs(stage, last)
             red.ag(stage, last - 1)
-        first = red.out_copies(last - 1, last - 1, rows_out, cols_out)
-        for copy in first:
+            if stage == 1:
+                for copy in outs[0]:
+                    copy.wait()
+        red.rs(4, last)
+        red.ag(0, last)
+        red.ag(4, last - 1)
+        for copy in outs[1]:
             copy.start()
-        for stage in range(5):
+        for stage in range(1, 5):
             red.ag(stage, last)
-        run(red.out_copies(last, last, rows_out, cols_out))
-        for copy in first:
+        run(outs[2])
+        for copy in outs[1]:
             copy.wait()
 
 
@@ -327,7 +360,7 @@
         def params(collective=None):
             if collective is None:
                 return pltpu.CompilerParams(vmem_limit_bytes=60 * 2**20)
-            return pltpu.CompilerParams(vmem_limit_bytes=62 * 2**20, collective_id=collective, has_side_effects=True)
+            return pltpu.CompilerParams(vmem_limit_bytes=63 * 2**20, collective_id=collective, has_side_effects=True)
 
         a_one, h_two = pl.pallas_call(
             forward_kernel,
@@ -343,18 +376,23 @@
             name="forward",
         )(x, w_one, w_two)
 
-        tile_spec = pl.BlockSpec((TILE, d), lambda j, r: (r, 0))
-        col_spec = pl.BlockSpec((TILE, side), lambda j, r: (r, j))
+        def tile_spec(tile):
+            return pl.BlockSpec((tile, d), lambda j, r: (r, 0))
+
+        def col_spec(tile):
+            return pl.BlockSpec((tile, side), lambda j, r: (r, j))
+
         w_spec = pl.BlockSpec((d, side), lambda j, r: (0, j))
+        back_spec = pl.BlockSpec((side, d), lambda j, r: (j, 0)) if TRANS_B else w_spec
 
         half_rows = jax.ShapeDtypeStruct((2 * side, d), F32)
         half_cols = jax.ShapeDtypeStruct((d, 2 * side), F32)
 
         d_a3, w4_a, w3_a, partial, pieces = pl.pallas_call(
-            functools.partial(upper_kernel, n_dev, steps),
-            grid=(CHUNKS, steps),
-            in_specs=[tile_spec, tile_spec, w_spec, w_spec],
-            out_specs=[col_spec] + [any_spec] * 4,
+            functools.partial(upper_kernel, n_dev, n // UP_TILE),
+            grid=(CHUNKS, n // UP_TILE),
+            in_specs=[tile_spec(UP_TILE), tile_spec(UP_TILE), w_spec, back_spec],
+            out_specs=[col_spec(UP_TILE)] + [any_spec] * 4,
             out_shape=[
                 jax.ShapeDtypeStruct((n, ff), BF16),
                 half_rows,
@@ -362,10 +400,10 @@
                 jax.ShapeDtypeStruct((2 * side, side), F32),
                 jax.ShapeDtypeStruct((COLORS, side // COLORS // 8, side), F32),
             ],
-            scratch_shapes=scratch(side),
+            scratch_shapes=[pltpu.VMEM((UP_TILE, side), BF16)] + scratch(side),
             compiler_params=params(0),
             name="upper",
-        )(h_two, g, w_three, w_four.T)
+        )(h_two, g, w_three, w_four if TRANS_B else w_four.T)
 
         d_h2, w4_b, w3_b = pl.pallas_call(
             functools.partial(middle_kernel, n_dev, steps),
@@ -385,15 +423,15 @@
         )(d_a3, w_three, g, partial, pieces)
 
         grad_w2, grad_w1 = pl.pallas_call(
-            functools.partial(lower_kernel, n_dev, steps),
-            grid=(CHUNKS, steps),
-            in_specs=[tile_spec, tile_spec, col_spec, w_spec],
+            functools.partial(lower_kernel, n_dev, n // LOW_TILE),
+            grid=(CHUNKS, n // LOW_TILE),
+            in_specs=[tile_spec(LOW_TILE), tile_spec(LOW_TILE), col_spec(LOW_TILE), back_spec],
             out_specs=[any_spec] * 2,
             out_shape=[jax.ShapeDtypeStruct((ff, d), F32), jax.ShapeDtypeStruct((d, ff), F32)],
-            scratch_shapes=scratch(side),
+            scratch_shapes=[pltpu.VMEM((LOW_TILE, side), BF16)] * 2 + scratch(side),
             compiler_params=params(2),
             name="lower",
-        )(x, d_h2, a_one, w_two.T)
+        )(x, d_h2, a_one, w_two if TRANS_B else w_two.T)
 
         grad_w4 = jnp.concatenate([w4_a, w4_b], axis=0)
         grad_w3 = jnp.concatenate([w3_a, w3_b], axis=1)

time: 679 us -> 619 us (0.912)
  Pallas kernels: 639 us -> 589 us
  local copies, waits for them, and re-layouts: 25.8 us -> 12.5 us
    pallas_call x2, Pallas kernels: 471 us -> 424 us  [the longest x1 215 us: device_step(): pl.pallas_call(functools.partial(lower_kernel, n_dev, n // LOW_TILE), gri...]
    unnamed x10 -> x8, local copies, waits for them, and re-layouts: 25.8 us -> 12.5 us
where the time goes in v2:
time: 619 us
  Pallas kernels  589 us (95%)
  other arithmetic  16.8 us (3%)
  local copies, waits for them, and re-layouts  12.5 us (2%)
    pallas_call x1, Pallas kernels, device_step(): pl.pallas_call(functools.partial(lower_kernel, n_dev, n // LOW_TILE), gri...  215 us
    pallas_call x1, Pallas kernels, device_step(): pl.pallas_call(functools.partial(upper_kernel, n_dev, n // UP_TILE), grid...  209 us
    pallas_call x1, Pallas kernels, device_step(): pl.pallas_call(forward_kernel, grid=(steps,), in_specs=[pl.BlockSpec((TIL...  92.1 us
    pallas_call x1, Pallas kernels, device_step(): pl.pallas_call(functools.partial(middle_kernel, n_dev, steps), grid=(step...  73.6 us
    unnamed x8, local copies, waits for them, and re-layouts  12.5 us

profile of v2, /device:TPU:0, one launch (start us, length us, event | category | flops | bytes accessed | tf_op | source)
XLA Modules:
  0.0 619.3 jit_solution(9153900368991170450)
XLA Ops:
  0.6 92.1 %forward.1 = (bf16[8192,3072]{1,0:T(8,128)(2,1)}, bf16[8192,768]{1,0:T(8,128)(2,1)}) custom-call(bf16[8192,768]{1,0:T(8,128)(2,1)} %x_ref.3, bf16[768,3072]{1,0:T(8,128)(2,1)} %w1_ref.1, bf16[3072,768]{1,0:T(8,128)(2,1)} %w2t_ref.1), custom_call_target="tpu_custom_call" | custom-call | tf_op jit(solution)/shard_map/forward/pallas_call | solution.py:365
  92.8 208.6 %upper.1 = (bf16[8192,3072]{1,0:T(8,128)(2,1)}, f32[1536,768]{1,0:T(8,128)}, f32[768,1536]{1,0:T(8,128)}, f32[1536,768]{1,0:T(8,128)}, f32[3,32,768]{2,1,0:T(8,128)}) custom-call(bf16[8192,768]{1,0:T(8,128)(2,1)} %get-tuple-element.16.h2_ref, bf16[8192,768]{1,0:T(8,128)(2,1)} %g_ref.3, bf16[768,3072]{1,0:T(8,128)(2,1)} %w3_ref.3, bf16[3072,768]{1,0:T(8,128)(2,1)} %w4t_ref.1), custom_call_target="tpu_custom_call" | custom-call | tf_op jit(solution)/shard_map/upper/pallas_call | solution.py:391
  301.3 73.6 %middle.1 = (bf16[8192,768]{1,0:T(8,128)(2,1)}, f32[1536,768]{1,0:T(8,128)}, f32[768,1536]{1,0:T(8,128)}) custom-call(bf16[8192,3072]{1,0:T(8,128)(2,1)} %get-tuple-element.17.da3_ref, bf16[768,3072]{1,0:T(8,128)(2,1)} %w3_ref.3, bf16[8192,768]{1,0:T(8,128)(2,1)} %g_ref.3, f32[1536,768]{1,0:T(8,128)} %get-tuple-element.18.partial_ref, ...), custom_call_target="tpu_custom_call" | custom-call | tf_op jit(solution)/shard_map/middle/pallas_call | solution.py:408
  375.0 214.9 %lower.1 = (f32[3072,768]{1,0:T(8,128)}, f32[768,3072]{1,0:T(8,128)}) custom-call(bf16[8192,768]{1,0:T(8,128)(2,1)} %x_ref.3, bf16[8192,768]{1,0:T(8,128)(2,1)} %get-tuple-element.20.dh2_ref, bf16[8192,3072]{1,0:T(8,128)(2,1)} %get-tuple-element.21.a1_ref, bf16[3072,768]{1,0:T(8,128)(2,1)} %w2t_ref.1), custom_call_target="tpu_custom_call" | custom-call | tf_op jit(solution)/shard_map/lower/pallas_call | solution.py:425
  589.9 8.6 %pad_maximum_fusion = f32[768,3072]{1,0:T(8,128)} fusion(f32[768,1536]{1,0:T(8,128)} %get-tuple-element.25, f32[768,1536]{1,0:T(8,128)} %get-tuple-element.24), kind=kLoop, calls=%fused_computation | loop fusion | flops 2359296 | bytes 18874368 | tf_op jit(solution)/shard_map/concatenate | solution.py:437
  598.5 0.0 slice-start
  598.5 0.0 slice-start.1
  598.5 8.3 %pad_maximum_fusion.1 = f32[3072,768]{1,0:T(8,128)} fusion(f32[1536,768]{1,0:T(8,128)} %get-tuple-element.27, f32[1536,768]{1,0:T(8,128)} %get-tuple-element.26), kind=kLoop, calls=%fused_computation.1 | loop fusion | flops 2359296 | bytes 18874368 | tf_op jit(solution)/shard_map/concatenate | solution.py:436
  606.8 0.0 slice-start.2
  606.8 8.8 %copy.12 = f32[768,3072]{1,0:T(8,128)} copy(f32[768,3072]{1,0:T(8,128)} %get-tuple-element.32) | data formatting | bytes 18874368
  615.5 0.0 slice-done
  615.5 0.0 slice-done.1
  615.5 0.0 slice-done.2
  615.5 3.7 copy.13
  (1 shorter events, 0.0 us)
Async XLA Ops:
  598.5 17.0 %slice-start = ((s8[9437184]{0:T(1024)(128)(4,1)}), s8[4194304]{0:T(1024)(128)(4,1)S(1)}, s32[]{:S(2)}) async-start(s8[9437184]{0:T(1024)(128)(4,1)} %bitcast), calls=%async_computation | async-start | bytes 8388608
  598.5 17.0 %slice-start.1 = ((s8[9437184]{0:T(1024)(128)(4,1)}), s8[1048576]{0:T(1024)(128)(4,1)S(1)}, s32[]{:S(2)}) async-start(s8[9437184]{0:T(1024)(128)(4,1)} %bitcast), calls=%async_computation.1 | async-start | bytes 2097152
  606.8 8.8 %slice-start.2 = ((s8[9437184]{0:T(1024)(128)(4,1)}), s8[4194304]{0:T(1024)(128)(4,1)S(1)}, s32[]{:S(2)}) async-start(s8[9437184]{0:T(1024)(128)(4,1)} %bitcast), calls=%async_computation.2 | async-start | bytes 8388608
